TPU v7x, 256 devices: a whole 4x4x8 slice. The times are simulated.
256 devices in a mesh: wide: 32 (over z_hi, y, core), shard: 8 (over z_lo, x).
Axes of the slice: x: 4, y: 4, z: 8 (z_hi: 4, z_lo: 2; z = z_hi * 2 + z_lo), core: 2. Of those that a mesh axis runs over, the one named last changes fastest.
Arguments:
- weights: bfloat16 [1024, 8192], P('shard'), may hold values from -6 to 6
- momentum: bfloat16 [32, 1024, 8192], P('wide', 'shard'), may hold values from -6 to 6
- grads: bfloat16 [2, 32, 1024, 8192], P(None, 'wide', 'shard'), may hold values from -6 to 6
- offsets: int32 [8, 64], P('shard'), may hold values from 0 to 96
- owners: int32 [8, 64], P('shard'), may hold values from 0 to 63, each once within a row
- exp_avg: float32 [8, 64, 32, 128], P('shard', 'wide'), may hold values from -7 to 7
- exp_sq: float32 [8, 64, 32, 128], P('shard', 'wide'), may hold values from 0.01 to 1
Outputs:
- new_weights: bfloat16 [1024, 8192], P('shard')
- new_momentum: bfloat16 [32, 1024, 8192], P('wide', 'shard')
- new_avg: float32 [8, 64, 32, 128], P('shard', 'wide')
- new_sq: float32 [8, 64, 32, 128], P('shard', 'wide')
- scales: float32 [2], replicated
Inputs may be any that keep to these rules, and one draw needn't show every extreme that they name: `offsets`: each block's band spans 32 consecutive transform rows. Each row of owners is a permutation of 0 to 63.
All inputs are finite; a program needn't handle non-finite values.
Results may differ from a plain program's by a relative error of at most 0.003.
Values may be sent and summed in bfloat16 or wider, within the bound.
A program may use at most 128 MiB of HBM per device.

v0:
```python
import functools
import jax
import jax.numpy as jnp
from jax import lax
from jax.sharding import Mesh
from jax.sharding import PartitionSpec as P

STEPS = 2
WIDE = ("wide_0", "wide_1", "wide_2")
SHARD = ("shard_0", "shard_1")
WIDE_SHARD = ("wide_0", "wide_1", "wide_2", "shard_0", "shard_1")
highest = lax.Precision.HIGHEST
momentum_decay = 0.9
beta_one = 0.8
beta_two = 0.95
adam_eps = 1e-08
rms_eps = 1e-06
learning_rate = 0.2


def one_axis_at_a_time(shard, axes):
    return functools.reduce(lax.psum, axes, shard)


def laid_out(parts, dim):
    parts = jnp.moveaxis(parts, 0, dim)
    lengths = parts.shape
    return parts.reshape(*lengths[:dim], lengths[dim] * lengths[dim + 1], *lengths[dim + 2 :])


def from_everyone(shard, axis):
    length = lax.axis_size(axis)
    return lax.all_to_all(
        jnp.broadcast_to(shard[None], (length, *shard.shape)), axis, 0, 0, tiled=True
    )


def gathered_copies(shard, axis, dim):
    return laid_out(from_everyone(shard, axis), dim)


def dct_table(length):
    frequency = jnp.arange(length, dtype=jnp.float32)[:, None]
    position = jnp.arange(length, dtype=jnp.float32)[None, :]
    cosines = jnp.cos(jnp.pi * (2.0 * position + 1.0) * frequency / (2.0 * length))
    scaling = jnp.where(frequency == 0.0, jnp.sqrt(1.0 / length), jnp.sqrt(2.0 / length))
    return cosines * scaling


def band_tables(basis, offsets, band_rows):
    indices = offsets[:, :, None] + jnp.arange(band_rows, dtype=jnp.int32)[None, None, :]
    return basis[indices]


def inverse(coefs, picked, basis):
    right_part = jnp.einsum("rjpc,cb->rjpb", coefs, basis, precision=highest)
    return jnp.einsum("rjpa,rjpb->rajb", picked, right_part, precision=highest)


def per_device(weights, momentum, grads, offsets, owners, exp_avg, exp_sq):
    block_len = exp_avg.shape[3]
    band_rows = exp_avg.shape[2]
    basis = dct_table(block_len)
    picked = band_tables(basis, offsets, band_rows)
    slot_order = jnp.argsort(owners, axis=1)
    row_blocks = offsets.shape[0]
    col_blocks = offsets.shape[1]
    block_shape = (row_blocks, block_len, col_blocks, block_len)
    replicas = lax.axis_size(WIDE)
    count_all = exp_avg.size * lax.axis_size(WIDE) * lax.axis_size(SHARD)
    weight_now = weights.astype(jnp.float32).reshape(block_shape)
    moment_now = momentum[0].astype(jnp.float32).reshape(block_shape)
    avg_now = exp_avg
    sq_now = exp_sq
    scales = []
    for step_index in range(STEPS):
        blended = momentum_decay * moment_now + grads[step_index, 0].astype(jnp.float32).reshape(
            block_shape
        )
        left_part = jnp.einsum("rjpa,rajb->rjpb", picked, blended, precision=highest)
        band_coef = jnp.einsum("rjpb,cb->rjpc", left_part, basis, precision=highest)
        moment_now = blended - inverse(band_coef, picked, basis)
        slot_band = jnp.take_along_axis(band_coef, slot_order[:, :, None, None], axis=1)
        pieces = lax.all_to_all(
            slot_band.astype(jnp.bfloat16), WIDE, split_axis=1, concat_axis=0, tiled=True
        ).astype(slot_band.dtype)
        summed = jnp.sum(pieces.reshape((replicas, row_blocks) + pieces.shape[1:]), axis=0)
        mean_band = summed / replicas
        avg_now = beta_one * avg_now + (1.0 - beta_one) * mean_band
        sq_now = beta_two * sq_now + (1.0 - beta_two) * mean_band * mean_band
        raw_update = avg_now / (jnp.sqrt(sq_now) + adam_eps)
        power_sum = one_axis_at_a_time(jnp.sum(raw_update * raw_update), WIDE_SHARD)
        spread = jnp.sqrt(power_sum / count_all + rms_eps)
        update = (raw_update / spread).astype(jnp.bfloat16)
        gathered = gathered_copies(update, WIDE, 1)
        block_update = jnp.take_along_axis(
            gathered.astype(jnp.float32), owners[:, :, None, None], axis=1
        )
        weight_now = weight_now - learning_rate * inverse(block_update, picked, basis)
        scales.append(spread)
    new_weights = weight_now.reshape(weights.shape).astype(jnp.bfloat16)
    new_momentum = moment_now.reshape(momentum.shape).astype(jnp.bfloat16)
    return (new_weights, new_momentum, avg_now, sq_now, jnp.stack(scales))


def solution(mesh):
    split = Mesh(
        mesh.devices.reshape(4, 4, 2, 2, 4), ("wide_0", "wide_1", "wide_2", "shard_0", "shard_1")
    )
    in_specs = (
        P(SHARD, None),
        P(WIDE, SHARD, None),
        P(None, WIDE, SHARD, None),
        P(SHARD, None),
        P(SHARD, None),
        P(SHARD, WIDE, None, None),
        P(SHARD, WIDE, None, None),
    )
    out_specs = (
        P(SHARD, None),
        P(WIDE, SHARD, None),
        P(SHARD, WIDE, None, None),
        P(SHARD, WIDE, None, None),
        P(),
    )
    return jax.shard_map(
        per_device, mesh=split, in_specs=in_specs, out_specs=out_specs, check_vma=False
    )
```

profile of v0, /device:TPU:1, one launch (start us, length us, event | category | flops | bytes accessed | tf_op | source)
XLA Modules:
  0.0 243.5 jit_solution(2718648643845490075)
XLA Ops:
  0.6 0.7 copy.36
  1.4 1.0 sort.17
  2.6 0.7 compare_select_fusion
  3.4 6.6 %slice_convert_fusion.1 = (f32[1,1,128,8192]{3,2,1,0:T(8,128)}, f32[16,8,64,128]{3,1,2,0:T(8,128)S(1)}, f32[1,1,128,8192]{3,2,1,0:T(8,128)}) fusion(bf16[2,1,128,8192]{3,2,1,0:T(8,128)(2,1)} %param.11), kind=kLoop, calls=%fused_computation.20 | loop fusion | flops 2097152 | bytes 16777216 | tf_op jit(solution)/shard_map/convert_element_type | solution.py:77
  10.0 2.7 %copy.49 = f32[16,8,64,128]{3,2,1,0:T(8,128)} copy(f32[16,8,64,128]{3,1,2,0:T(8,128)S(1)} %get-tuple-element.42) | data formatting | bytes 8388608
  12.7 2.5 %convert_multiply_fusion = (f32[1,128,8192]{2,1,0:T(8,128)}, f32[16,8,64,128]{3,1,2,0:T(8,128)S(1)}) fusion(bf16[1,128,8192]{2,1,0:T(8,128)(2,1)S(1)} %copy-done.2), kind=kLoop, calls=%fused_computation.18 | loop fusion | flops 2097152 | bytes 10485760 | tf_op jit(solution)/shard_map/mul | solution.py:77
  15.3 2.7 %copy.48 = f32[16,8,64,128]{3,2,1,0:T(8,128)} copy(f32[16,8,64,128]{3,1,2,0:T(8,128)S(1)} %get-tuple-element.45) | data formatting | bytes 8388608
  17.9 0.2 cosine_multiply_fusion
  18.2 6.0 %gather_fusion = f32[2048,128]{1,0:T(8,128)S(1)} fusion(f32[128,128]{1,0:T(8,128)S(1)} %cosine_multiply_fusion, s32[2048]{0:T(1024)S(1)} %broadcast_clamp_fusion), kind=kCustom, calls=%fused_computation.4 | custom fusion | bytes 2105344 | tf_op jit(solution)/shard_map/gather | solution.py:52
  24.2 12.7 %fusion.6 = f32[64,32,128]{2,1,0:T(8,128)S(1)} fusion(f32[64,32,128]{2,1,0:T(8,128)S(1)} %bitcast.181, f32[128,64,128]{2,1,0:T(8,128)} %bitcast.188, f32[128,64,128]{2,1,0:T(8,128)} %bitcast.189), kind=kOutput, calls=%fused_computation.16 | convolution fusion | flops 403701760 | bytes 10485760 | tf_op jit(solution)/shard_map/rjpa,rajb->rjpb/dot_general | solution.py:80
  36.9 1.2 fusion.30
  38.1 1.2 fusion.27
  39.3 5.6 %copy.41 = f32[1,1,128,8192]{2,3,1,0:T(8,128)} copy(f32[1,1,128,8192]{3,2,1,0:T(8,128)} %get-tuple-element.41) | data formatting | bytes 8388608 | tf_op jit(solution)/shard_map/convert_element_type | solution.py:77
  44.9 5.6 %copy.42 = f32[1,1,128,8192]{2,3,1,0:T(8,128)} copy(f32[1,1,128,8192]{3,2,1,0:T(8,128)} %get-tuple-element.43) | data formatting | bytes 8388608 | tf_op jit(solution)/shard_map/convert_element_type | solution.py:77
  50.5 5.6 %copy.40 = f32[1,128,8192]{1,2,0:T(8,128)} copy(f32[1,128,8192]{2,1,0:T(8,128)} %get-tuple-element.44) | data formatting | bytes 8388608 | tf_op jit(solution)/shard_map/mul | solution.py:77
  56.1 10.1 %fusion.3 = f32[1,128,64,128]{1,3,2,0:T(8,128)S(1)} fusion(f32[1,128,64,128]{1,3,2,0:T(8,128)} %bitcast.191, f32[1,128,64,128]{1,3,2,0:T(8,128)} %bitcast.192, f32[1,128,64,128]{1,3,2,0:T(8,128)} %bitcast.190, f32[64,32,128]{2,1,0:T(8,128)S(1)} %fusion.27, f32[64,32,128]{2,1,0:T(8,128)S(1)} %bitcast.182), kind=kOutput, calls=%fused_computation.11 | convolution fusion | flops 406847488 | bytes 18874368 | tf_op jit(solution)/shard_map/rjpa,rjpb->rajb/dot_general | solution.py:57
  66.2 6.7 %fusion.4 = f32[64,32,128]{2,1,0:T(8,128)S(1)} fusion(f32[64,32,128]{2,1,0:T(8,128)S(1)} %bitcast.183, f32[1,128,64,128]{1,3,2,0:T(8,128)S(1)} %fusion.3), kind=kOutput, calls=%fused_computation.13 | convolution fusion | flops 402653184 | bytes 6291456 | tf_op jit(solution)/shard_map/rjpa,rajb->rjpb/dot_general | solution.py:80
  72.8 1.2 fusion.25
  74.1 1.4 gather_fusion.1
  75.6 0.7 gather_fusion.3
  76.2 2.1 fusion.17
  78.3 30.7 %all_to_all.28 = bf16[1,64,32,128]{3,2,0,1:T(8,128)(2,1)S(1)} all-to-all(bf16[1,64,32,128]{3,2,0,1:T(8,128)(2,1)S(1)} %get-tuple-element.47), channel_id=1, replica_groups=mesh['wide_0'=4,'wide_1'=4,'wide_2'=2,'shard_0'=2,'shard_1'=4] {'wide_0'..., dimensions={1} | all-to-all | bytes 1048576 | tf_op jit(solution)/shard_map/all_to_all | solution.py:84
  109.0 4.2 %all-to-all-start = ((bf16[1,64,32,128]{3,2,0,1:T(8,128)(2,1)}), bf16[1,64,32,128]{3,2,0,1:T(8,128)(2,1)S(1)}, u32[]{:S(2)}, u32[]{:S(2)}) async-start(bf16[1,64,32,128]{3,2,0,1:T(8,128)(2,1)} %get-tuple-element.48), calls=%async_computation | async-start | bytes 1048576 | tf_op jit(solution)/shard_map/all_to_all | solution.py:84
  113.3 17.1 %all-to-all-done = bf16[1,64,32,128]{3,2,0,1:T(8,128)(2,1)S(1)} async-done(((bf16[1,64,32,128]{3,2,0,1:T(8,128)(2,1)}), bf16[1,64,32,128]{3,2,0,1:T(8,128)(2,1)S(1)}, u32[]{:S(2)}, u32[]{:S(2)}) %all-to-all-start) | async-done | bytes 524320 | tf_op jit(solution)/shard_map/all_to_all | solution.py:84
  130.6 0.7 multiply_reduce_fusion
  131.2 9.8 %all-reduce.2 = (f32[]{:T(128)}, f32[]{:T(128)}) all-reduce(f32[]{:T(128)} %get-tuple-element.46, f32[]{:T(128)} %get-tuple-element.38), channel_id=1, replica_groups=mesh['wide_0'=4,'wide_1'=4,'wide_2'=2,'shard_0'=2,'shard_1'=4] {'wide_0'}, use_global_device_ids=true, to_apply=%region_3.5 | all-reduce | flops 2 | bytes 16 | tf_op jit(solution)/shard_map/psum | solution.py:22
  141.1 7.8 %all-reduce.1 = (f32[]{:T(128)}, f32[]{:T(128)}) all-reduce(f32[]{:T(128)} %get-tuple-element.32, f32[]{:T(128)} %get-tuple-element.33), channel_id=1, replica_groups=mesh['wide_0'=4,'wide_1'=4,'wide_2'=2,'shard_0'=2,'shard_1'=4] {'wide_1'}, use_global_device_ids=true, to_apply=%region_4.6 | all-reduce | flops 2 | bytes 16 | tf_op jit(solution)/shard_map/psum | solution.py:22
  148.9 6.8 %all-reduce.4 = (f32[]{:T(128)}, f32[]{:T(128)}) all-reduce(f32[]{:T(128)} %get-tuple-element.30, f32[]{:T(128)} %get-tuple-element.31), channel_id=1, replica_groups=mesh['wide_0'=4,'wide_1'=4,'wide_2'=2,'shard_0'=2,'shard_1'=4] {'wide_2'}, use_global_device_ids=true, to_apply=%region_5.7 | all-reduce | flops 2 | bytes 16 | tf_op jit(solution)/shard_map/psum | solution.py:22
  155.7 4.4 %all-reduce.3 = (f32[]{:T(128)}, f32[]{:T(128)}) all-reduce(f32[]{:T(128)} %get-tuple-element.36, f32[]{:T(128)} %get-tuple-element.37), channel_id=1, replica_groups=mesh['wide_0'=4,'wide_1'=4,'wide_2'=2,'shard_0'=2,'shard_1'=4] {'shard_0'}, use_global_device_ids=true, to_apply=%region_6.8 | all-reduce | flops 2 | bytes 16 | tf_op jit(solution)/shard_map/psum | solution.py:22
  160.1 9.1 %all-reduce = (f32[]{:T(128)}, f32[]{:T(128)}) all-reduce(f32[]{:T(128)} %get-tuple-element.34, f32[]{:T(128)} %get-tuple-element.35), channel_id=1, replica_groups=mesh['wide_0'=4,'wide_1'=4,'wide_2'=2,'shard_0'=2,'shard_1'=4] {'shard_1'}, use_global_device_ids=true, to_apply=%region_7.9 | all-reduce | flops 2 | bytes 16 | tf_op jit(solution)/shard_map/psum | solution.py:22
  169.9 0.9 broadcast_in_dim.50
  170.8 7.6 %all-to-all-start.3 = ((bf16[32,1,2,32,128]{4,3,2,1,0:T(8,128)(2,1)}), bf16[32,1,2,32,128]{4,3,2,1,0:T(8,128)(2,1)S(1)}, u32[]{:S(2)}, u32[]{:S(2)}) async-start(bf16[32,1,2,32,128]{4,3,2,1,0:T(8,128)(2,1)} %broadcast_in_dim.50), calls=%async_computation.3 | async-start | bytes 1048576 | tf_op jit(solution)/shard_map/all_to_all | solution.py:33
  178.4 2.2 fusion.22
  181.3 14.0 %all-to-all-done.3 = bf16[32,1,2,32,128]{4,3,2,1,0:T(8,128)(2,1)S(1)} async-done(((bf16[32,1,2,32,128]{4,3,2,1,0:T(8,128)(2,1)}), bf16[32,1,2,32,128]{4,3,2,1,0:T(8,128)(2,1)S(1)}, u32[]{:S(2)}, u32[]{:S(2)}) %all-to-all-start.3) | async-done | bytes 524320 | tf_op jit(solution)/shard_map/all_to_all | solution.py:33
  195.3 1.0 broadcast_in_dim.47
  196.2 5.8 %all-to-all-start.1 = ((bf16[32,1,2,32,128]{4,3,2,1,0:T(8,128)(2,1)}), bf16[32,1,2,32,128]{4,3,2,1,0:T(8,128)(2,1)}, u32[]{:S(2)}, u32[]{:S(2)}) async-start(bf16[32,1,2,32,128]{4,3,2,1,0:T(8,128)(2,1)} %broadcast_in_dim.47), calls=%async_computation.1 | async-start | bytes 1048576 | tf_op jit(solution)/shard_map/all_to_all | solution.py:33
  202.1 8.7 %fusion = bf16[1,128,64,128]{1,3,2,0:T(8,128)(2,1)S(1)} fusion(f32[1,128,64,128]{1,3,2,0:T(8,128)} %copy-done, f32[64,32,128]{2,1,0:T(8,128)} %fusion.22, f32[64,32,128]{2,1,0:T(8,128)S(1)} %bitcast.184), kind=kOutput, calls=%fused_computation.6 | convolution fusion | flops 404750336 | bytes 8388608 | tf_op jit(solution)/shard_map/rjpa,rjpb->rajb/dot_general | solution.py:57
  210.8 2.9 %copy.46 = bf16[1,128,8192]{2,1,0:T(8,128)(2,1)} copy(bf16[1,128,8192]{1,2,0:T(8,128)(2,1)S(1)} %bitcast.194) | data formatting | bytes 4194304
  213.7 4.3 %copy.35 = f32[128,8192]{0,1:T(8,128)} copy(bf16[128,8192]{1,0:T(8,128)(2,1)} %param.9) | data formatting | bytes 6291456 | tf_op jit(solution)/shard_map/reshape | solution.py:71
  218.1 0.6 pad_maximum_fusion
  218.8 0.6 gather_fusion.4
  219.5 1.2 bitcast_convert_fusion.1
  220.6 1.6 gather_fusion.2
  222.2 1.2 fusion.8
  223.5 2.6 %fusion.11 = f32[64,32,128]{2,1,0:T(8,128)S(1)} fusion(f32[64,32,128]{2,1,0:T(8,128)} %gather_fusion.2, pred[64]{0:T(512)(128)(4,1)S(1)} %and_bitcast_fusion, f32[128]{0:T(128)S(1)} %get-tuple-element.49, f32[128]{0:T(128)S(1)} %get-tuple-element.50), kind=kOutput, calls=%fused_computation.28 | convolution fusion | flops 402964480 | bytes 2098240 | tf_op jit(solution)/shard_map/rjpc,cb->rjpb/dot_general | solution.py:56
  226.1 6.7 %fusion.62 = f32[64,128,128]{2,1,0:T(8,128)S(1)} fusion(f32[64,32,128]{2,1,0:T(8,128)S(1)} %fusion.11, f32[64,32,128]{2,1,0:T(8,128)S(1)} %bitcast.185), kind=kOutput, calls=%fused_computation.105 | convolution fusion | flops 402653184 | bytes 6291456 | tf_op jit(solution)/shard_map/rjpa,rjpb->rajb/dot_general | solution.py:57
  232.8 7.4 %fusion.1 = bf16[1,128,64,128]{1,3,2,0:T(8,128)(2,1)S(1)} fusion(f32[1,128,64,128]{1,3,2,0:T(8,128)S(1)} %bitcast.187, f32[64,128,128]{2,1,0:T(8,128)S(1)} %fusion.62, f32[64,32,128]{2,1,0:T(8,128)S(1)} %fusion.8, f32[64,32,128]{2,1,0:T(8,128)S(1)} %bitcast.186), kind=kOutput, calls=%fused_computation.8 | convolution fusion | flops 407896064 | bytes 12582912 | tf_op jit(solution)/shard_map/rjpa,rjpb->rajb/dot_general | solution.py:57
  240.2 2.9 %copy.45 = bf16[128,8192]{1,0:T(8,128)(2,1)} copy(bf16[128,8192]{0,1:T(8,128)(2,1)S(1)} %bitcast.193) | data formatting | bytes 4194304
  (37 shorter events, 0.7 us)
Async XLA Ops:
  10.0 2.7 %copy-start.2 = (bf16[1,128,8192]{2,1,0:T(8,128)(2,1)S(1)}, bf16[1,128,8192]{2,1,0:T(8,128)(2,1)}, u32[]{:S(2)}) copy-start(bf16[1,128,8192]{2,1,0:T(8,128)(2,1)} %param.10) | copy-start | bytes 6291460
  66.2 7.9 %copy-start = (f32[1,128,64,128]{1,3,2,0:T(8,128)}, f32[1,128,64,128]{1,3,2,0:T(8,128)S(1)}, u32[]{:S(2)}) copy-start(f32[1,128,64,128]{1,3,2,0:T(8,128)S(1)} %fusion.3) | copy-start | bytes 12582916
  74.1 56.4 %copy-start.5 = (f32[1,2,32,128]{3,2,1,0:T(8,128)S(1)}, f32[1,2,32,128]{3,2,1,0:T(8,128)}, u32[]{:S(2)}) copy-start(f32[1,2,32,128]{3,2,1,0:T(8,128)} %param.15) | copy-start | bytes 98308
  74.1 56.4 %copy-start.6 = (f32[1,2,32,128]{3,2,1,0:T(8,128)S(1)}, f32[1,2,32,128]{3,2,1,0:T(8,128)}, u32[]{:S(2)}) copy-start(f32[1,2,32,128]{3,2,1,0:T(8,128)} %param.14) | copy-start | bytes 98308
  109.0 21.4 %all-to-all-start = ((bf16[1,64,32,128]{3,2,0,1:T(8,128)(2,1)}), bf16[1,64,32,128]{3,2,0,1:T(8,128)(2,1)S(1)}, u32[]{:S(2)}, u32[]{:S(2)}) async-start(bf16[1,64,32,128]{3,2,0,1:T(8,128)(2,1)} %get-tuple-element.48), calls=%async_computation | async-start | bytes 1048576 | tf_op jit(solution)/shard_map/all_to_all | solution.py:84
  131.2 79.6 %copy-start.7 = (f32[1,2,32,128]{3,2,1,0:T(8,128)}, f32[1,2,32,128]{3,2,1,0:T(8,128)S(1)}, u32[]{:S(2)}) copy-start(f32[1,2,32,128]{3,2,1,0:T(8,128)S(1)} %get-tuple-element.39) | copy-start | bytes 98308
  131.2 79.6 %copy-start.8 = (f32[1,2,32,128]{3,2,1,0:T(8,128)}, f32[1,2,32,128]{3,2,1,0:T(8,128)S(1)}, u32[]{:S(2)}) copy-start(f32[1,2,32,128]{3,2,1,0:T(8,128)S(1)} %get-tuple-element.40) | copy-start | bytes 98308
  170.8 24.5 %all-to-all-start.3 = ((bf16[32,1,2,32,128]{4,3,2,1,0:T(8,128)(2,1)}), bf16[32,1,2,32,128]{4,3,2,1,0:T(8,128)(2,1)S(1)}, u32[]{:S(2)}, u32[]{:S(2)}) async-start(bf16[32,1,2,32,128]{4,3,2,1,0:T(8,128)(2,1)} %broadcast_in_dim.50), calls=%async_computation.3 | async-start | bytes 1048576 | tf_op jit(solution)/shard_map/all_to_all | solution.py:33
  195.3 1.0 copy-start.3
  196.2 23.2 %all-to-all-start.1 = ((bf16[32,1,2,32,128]{4,3,2,1,0:T(8,128)(2,1)}), bf16[32,1,2,32,128]{4,3,2,1,0:T(8,128)(2,1)}, u32[]{:S(2)}, u32[]{:S(2)}) async-start(bf16[32,1,2,32,128]{4,3,2,1,0:T(8,128)(2,1)} %broadcast_in_dim.47), calls=%async_computation.1 | async-start | bytes 1048576 | tf_op jit(solution)/shard_map/all_to_all | solution.py:33
  213.7 4.4 %copy-start.9 = (s32[1,64]{1,0:T(1,128)S(1)}, s32[1,64]{1,0:T(1,128)}, u32[]{:S(2)}) copy-start(s32[1,64]{1,0:T(1,128)} %param.13) | copy-start | bytes 772
  213.7 5.0 %copy-start.4 = (bf16[32,1,2,32,128]{4,3,2,1,0:T(8,128)(2,1)S(1)}, bf16[32,1,2,32,128]{4,3,2,1,0:T(8,128)(2,1)}, u32[]{:S(2)}) copy-start(bf16[32,1,2,32,128]{4,3,2,1,0:T(8,128)(2,1)} %copy-done.3) | copy-start | bytes 1572868
  223.5 9.3 %copy-start.1 = (f32[128,8192]{0,1:T(8,128)S(1)}, f32[128,8192]{0,1:T(8,128)}, u32[]{:S(2)}) copy-start(f32[128,8192]{0,1:T(8,128)} %copy.35) | copy-start | bytes 12582916
where the time goes:
time: 248 us; the launch traced here: 244 us
  blocking collectives  68.6 us (28%)
  matrix products  61.9 us (25%)
  local copies, waits for them, and re-layouts  45.3 us (18%)
  waiting for transfers between devices  31.1 us (13%)
  starting transfers between devices  17.7 us (7%)
  other arithmetic  16.3 us (7%)
  between operations  2.73 us (1%)
    psum x5, blocking collectives, one_axis_at_a_time(): return functools.reduce(lax.psum, axes, shard)  37.9 us
    dot_general x4, matrix products, inverse(): return jnp.einsum('rjpa,rjpb->rajb', picked, right_part, precision=highest)  32.9 us
    all_to_all x1, blocking collectives, per_device(): lax.all_to_all(slot_band.astype(jnp.bfloat16), WIDE, split_axis=1, concat...  30.7 us
    dot_general x2, matrix products, per_device(): jnp.einsum('rjpa,rajb->rjpb', picked, blended, precision=highest)  19.4 us
    all_to_all x1, waiting for transfers between devices, per_device(): lax.all_to_all(slot_band.astype(jnp.bfloat16), WIDE, split_axis=1, concat...  17.1 us
    all_to_all x2, waiting for transfers between devices, from_everyone(): lax.all_to_all(jnp.broadcast_to(shard[None], (length, *shard.shape)), axi...  14 us
    all_to_all x2, starting transfers between devices, from_everyone(): lax.all_to_all(jnp.broadcast_to(shard[None], (length, *shard.shape)), axi...  13.4 us
    unnamed x25, local copies, waits for them, and re-layouts  11.9 us
  transfers between devices with their start and end apart: 3, of which 2 were waited for; matrix products, arithmetic and copies ran while one was open for 8% of the time, Pallas kernels for 0%

commit v1 on v0

--- a/solution.py
+++ b/solution.py
@@ -16,6 +16,22 @@
 adam_eps = 1e-08
 rms_eps = 1e-06
 learning_rate = 0.2
+
+
+def draw_the_group(obj, device_axis):
+    met_up = lax.psum(1, axis_name=device_axis)
+    return jnp.concatenate(
+        lax.all_to_all(
+            jnp.stack(jnp.split(obj, met_up, axis=1)),
+            axis_name=device_axis,
+            split_axis=0,
+            concat_axis=0,
+        ),
+        axis=0,
+    )
+
+
+_make_row = functools.partial(draw_the_group, device_axis=WIDE)
 
 
 def one_axis_at_a_time(shard, axes):
@@ -81,9 +97,7 @@
         band_coef = jnp.einsum("rjpb,cb->rjpc", left_part, basis, precision=highest)
         moment_now = blended - inverse(band_coef, picked, basis)
         slot_band = jnp.take_along_axis(band_coef, slot_order[:, :, None, None], axis=1)
-        pieces = lax.all_to_all(
-            slot_band.astype(jnp.bfloat16), WIDE, split_axis=1, concat_axis=0, tiled=True
-        ).astype(slot_band.dtype)
+        pieces = _make_row(slot_band.astype(jnp.bfloat16)).astype(slot_band.dtype)
         summed = jnp.sum(pieces.reshape((replicas, row_blocks) + pieces.shape[1:]), axis=0)
         mean_band = summed / replicas
         avg_now = beta_one * avg_now + (1.0 - beta_one) * mean_band

time: 248 us -> 276 us (1.11)
  local copies, waits for them, and re-layouts: 45.3 us -> 84.3 us
  blocking collectives: 68.6 us -> 37.2 us
  starting transfers between devices: 17.7 us -> 36.3 us
    unnamed x25 -> x87, local copies, waits for them, and re-layouts: 11.9 us -> 49.5 us
    all_to_all x1 -> x0, blocking collectives: 30.7 us -> none  [per_device(): lax.all_to_all(slot_band.astype(jnp.bfloat16), WIDE, split_axis=1, concat...]
    all_to_all x1 -> x2, starting transfers between devices: 4.24 us -> 22.5 us  [draw_the_group(): lax.all_to_all(jnp.stack(jnp.split(obj, met_up, axis=1)), axis_name=devic...]
    all_to_all x1 -> x2, waiting for transfers between devices: 17.1 us -> 18.1 us  [draw_the_group(): lax.all_to_all(jnp.stack(jnp.split(obj, met_up, axis=1)), axis_name=devic...]
  transfers between devices with their start and end apart: 3 -> 4, of which waited for: 2 -> 3; matrix products, arithmetic and copies ran while one was open for 8% -> 14% of each run, Pallas kernels for 0% -> 0%
where the time goes in v1:
time: 276 us; the launch traced here: 272 us
  local copies, waits for them, and re-layouts  84.3 us (31%)
  matrix products  61.9 us (22%)
  blocking collectives  37.2 us (13%)
  starting transfers between devices  36.3 us (13%)
  waiting for transfers between devices  33.8 us (12%)
  other arithmetic  15.5 us (6%)
  between operations  2.84 us (1%)
    unnamed x87, local copies, waits for them, and re-layouts  49.5 us
    psum x5, blocking collectives, one_axis_at_a_time(): return functools.reduce(lax.psum, axes, shard)  37.2 us
    dot_general x4, matrix products, inverse(): return jnp.einsum('rjpa,rjpb->rajb', picked, right_part, precision=highest)  32.9 us
    all_to_all x2, starting transfers between devices, draw_the_group(): lax.all_to_all(jnp.stack(jnp.split(obj, met_up, axis=1)), axis_name=devic...  22.5 us
    dot_general x2, matrix products, per_device(): jnp.einsum('rjpa,rajb->rjpb', picked, blended, precision=highest)  19.4 us
    all_to_all x2, waiting for transfers between devices, draw_the_group(): lax.all_to_all(jnp.stack(jnp.split(obj, met_up, axis=1)), axis_name=devic...  18.1 us
    all_to_all x2, waiting for transfers between devices, from_everyone(): lax.all_to_all(jnp.broadcast_to(shard[None], (length, *shard.shape)), axi...  15.8 us
    all_to_all x2, starting transfers between devices, from_everyone(): lax.all_to_all(jnp.broadcast_to(shard[None], (length, *shard.shape)), axi...  13.8 us
  transfers between devices with their start and end apart: 4, of which 3 were waited for; matrix products, arithmetic and copies ran while one was open for 14% of the time, Pallas kernels for 0%

profile of v1, /device:TPU:1, one launch (start us, length us, event | category | flops | bytes accessed | tf_op | source)
XLA Modules:
  0.0 271.9 jit_solution(11202984502190465715)
XLA Ops:
  0.6 0.7 copy.26
  1.4 1.0 sort.17
  2.6 0.7 compare_select_fusion
  3.4 6.6 %slice_convert_fusion.1 = (f32[1,1,128,8192]{3,2,1,0:T(8,128)}, f32[16,8,64,128]{3,1,2,0:T(8,128)S(1)}, f32[1,1,128,8192]{3,2,1,0:T(8,128)}) fusion(bf16[2,1,128,8192]{3,2,1,0:T(8,128)(2,1)} %param.11), kind=kLoop, calls=%fused_computation.20 | loop fusion | flops 2097152 | bytes 16777216 | tf_op jit(solution)/shard_map/convert_element_type | solution.py:93
  10.0 2.7 copy.37
  12.7 2.5 convert_multiply_fusion
  15.3 2.7 copy.36
  18.2 6.0 %gather_fusion = f32[2048,128]{1,0:T(8,128)S(1)} fusion(f32[128,128]{1,0:T(8,128)S(1)} %cosine_multiply_fusion, s32[2048]{0:T(1024)S(1)} %broadcast_clamp_fusion), kind=kCustom, calls=%fused_computation.4 | custom fusion | bytes 2105344 | tf_op jit(solution)/shard_map/gather | solution.py:68
  24.2 12.7 %fusion.6 = f32[64,32,128]{2,1,0:T(8,128)S(1)} fusion(f32[64,32,128]{2,1,0:T(8,128)S(1)} %bitcast.425, f32[128,64,128]{2,1,0:T(8,128)} %bitcast.432, f32[128,64,128]{2,1,0:T(8,128)} %bitcast.433), kind=kOutput, calls=%fused_computation.16 | convolution fusion | flops 403701760 | bytes 10485760 | tf_op jit(solution)/shard_map/rjpa,rajb->rjpb/dot_general | solution.py:96
  36.9 1.2 fusion.28
  38.1 1.2 fusion.25
  39.3 5.6 %copy.30 = f32[1,1,128,8192]{2,3,1,0:T(8,128)} copy(f32[1,1,128,8192]{3,2,1,0:T(8,128)} %get-tuple-element.36) | data formatting | bytes 8388608 | tf_op jit(solution)/shard_map/convert_element_type | solution.py:93
  44.9 5.6 %copy.31 = f32[1,1,128,8192]{2,3,1,0:T(8,128)} copy(f32[1,1,128,8192]{3,2,1,0:T(8,128)} %get-tuple-element.38) | data formatting | bytes 8388608 | tf_op jit(solution)/shard_map/convert_element_type | solution.py:93
  50.5 5.6 %copy.29 = f32[1,128,8192]{1,2,0:T(8,128)} copy(f32[1,128,8192]{2,1,0:T(8,128)} %get-tuple-element.39) | data formatting | bytes 8388608 | tf_op jit(solution)/shard_map/mul | solution.py:93
  56.1 10.1 %fusion.3 = f32[1,128,64,128]{1,3,2,0:T(8,128)S(1)} fusion(f32[1,128,64,128]{1,3,2,0:T(8,128)} %bitcast.435, f32[1,128,64,128]{1,3,2,0:T(8,128)} %bitcast.436, f32[1,128,64,128]{1,3,2,0:T(8,128)} %bitcast.434, f32[64,32,128]{2,1,0:T(8,128)S(1)} %fusion.25, f32[64,32,128]{2,1,0:T(8,128)S(1)} %bitcast.426), kind=kOutput, calls=%fused_computation.11 | convolution fusion | flops 406847488 | bytes 18874368 | tf_op jit(solution)/shard_map/rjpa,rjpb->rajb/dot_general | solution.py:73
  66.2 6.7 %fusion.4 = f32[64,32,128]{2,1,0:T(8,128)S(1)} fusion(f32[64,32,128]{2,1,0:T(8,128)S(1)} %bitcast.427, f32[1,128,64,128]{1,3,2,0:T(8,128)S(1)} %fusion.3), kind=kOutput, calls=%fused_computation.13 | convolution fusion | flops 402653184 | bytes 6291456 | tf_op jit(solution)/shard_map/rjpa,rajb->rjpb/dot_general | solution.py:96
  72.8 1.2 fusion.23
  74.1 1.4 gather_fusion.1
  75.5 0.7 gather_fusion.3
  76.2 1.3 fusion.10
  77.5 0.6 constant_dynamic-update-slice_fusion.31
  96.9 12.7 %all-to-all-start = ((bf16[32,1,2,32,128]{4,3,2,1,0:T(8,128)(2,1)}), bf16[32,1,2,32,128]{4,3,2,1,0:T(8,128)(2,1)S(1)}, u32[]{:S(2)}, u32[]{:S(2)}) async-start(bf16[32,1,2,32,128]{4,3,2,1,0:T(8,128)(2,1)} %constant_dynamic-update-slice_fusion), calls=%async_computation | async-start | bytes 1048576 | tf_op jit(solution)/shard_map/all_to_all | solution.py:24
  109.7 0.6 constant_dynamic-update-slice_fusion.63
  129.1 9.8 %all-to-all-start.2 = ((bf16[32,1,2,32,128]{4,3,2,1,0:T(8,128)(2,1)}), bf16[32,1,2,32,128]{4,3,2,1,0:T(8,128)(2,1)S(1)}, u32[]{:S(2)}, u32[]{:S(2)}) async-start(bf16[32,1,2,32,128]{4,3,2,1,0:T(8,128)(2,1)} %constant_dynamic-update-slice_fusion.32), calls=%async_computation.2 | async-start | bytes 1048576 | tf_op jit(solution)/shard_map/all_to_all | solution.py:24
  139.0 18.1 %all-to-all-done.2 = bf16[32,1,2,32,128]{4,3,2,1,0:T(8,128)(2,1)S(1)} async-done(((bf16[32,1,2,32,128]{4,3,2,1,0:T(8,128)(2,1)}), bf16[32,1,2,32,128]{4,3,2,1,0:T(8,128)(2,1)S(1)}, u32[]{:S(2)}, u32[]{:S(2)}) %all-to-all-start.2) | async-done | bytes 524320 | tf_op jit(solution)/shard_map/all_to_all | solution.py:24
  157.2 0.7 multiply_reduce_fusion
  157.8 9.0 %all-reduce.2 = (f32[]{:T(128)}, f32[]{:T(128)}) all-reduce(f32[]{:T(128)} %get-tuple-element.41, f32[]{:T(128)} %get-tuple-element.33), channel_id=1, replica_groups=mesh['wide_0'=4,'wide_1'=4,'wide_2'=2,'shard_0'=2,'shard_1'=4] {'wide_0'}, use_global_device_ids=true, to_apply=%region_3.5 | all-reduce | flops 2 | bytes 16 | tf_op jit(solution)/shard_map/psum | solution.py:38
  166.8 8.0 %all-reduce.1 = (f32[]{:T(128)}, f32[]{:T(128)}) all-reduce(f32[]{:T(128)} %get-tuple-element.27, f32[]{:T(128)} %get-tuple-element.28), channel_id=1, replica_groups=mesh['wide_0'=4,'wide_1'=4,'wide_2'=2,'shard_0'=2,'shard_1'=4] {'wide_1'}, use_global_device_ids=true, to_apply=%region_4.6 | all-reduce | flops 2 | bytes 16 | tf_op jit(solution)/shard_map/psum | solution.py:38
  174.8 6.6 %all-reduce.4 = (f32[]{:T(128)}, f32[]{:T(128)}) all-reduce(f32[]{:T(128)} %get-tuple-element.25, f32[]{:T(128)} %get-tuple-element.26), channel_id=1, replica_groups=mesh['wide_0'=4,'wide_1'=4,'wide_2'=2,'shard_0'=2,'shard_1'=4] {'wide_2'}, use_global_device_ids=true, to_apply=%region_5.7 | all-reduce | flops 2 | bytes 16 | tf_op jit(solution)/shard_map/psum | solution.py:38
  181.4 4.4 %all-reduce.3 = (f32[]{:T(128)}, f32[]{:T(128)}) all-reduce(f32[]{:T(128)} %get-tuple-element.31, f32[]{:T(128)} %get-tuple-element.32), channel_id=1, replica_groups=mesh['wide_0'=4,'wide_1'=4,'wide_2'=2,'shard_0'=2,'shard_1'=4] {'shard_0'}, use_global_device_ids=true, to_apply=%region_6.8 | all-reduce | flops 2 | bytes 16 | tf_op jit(solution)/shard_map/psum | solution.py:38
  185.8 9.2 %all-reduce = (f32[]{:T(128)}, f32[]{:T(128)}) all-reduce(f32[]{:T(128)} %get-tuple-element.29, f32[]{:T(128)} %get-tuple-element.30), channel_id=1, replica_groups=mesh['wide_0'=4,'wide_1'=4,'wide_2'=2,'shard_0'=2,'shard_1'=4] {'shard_1'}, use_global_device_ids=true, to_apply=%region_7.9 | all-reduce | flops 2 | bytes 16 | tf_op jit(solution)/shard_map/psum | solution.py:38
  195.8 0.9 broadcast_in_dim.50
  196.7 8.9 %all-to-all-start.3 = ((bf16[32,1,2,32,128]{4,3,2,1,0:T(8,128)(2,1)}), bf16[32,1,2,32,128]{4,3,2,1,0:T(8,128)(2,1)S(1)}, u32[]{:S(2)}, u32[]{:S(2)}) async-start(bf16[32,1,2,32,128]{4,3,2,1,0:T(8,128)(2,1)} %broadcast_in_dim.50), calls=%async_computation.3 | async-start | bytes 1048576 | tf_op jit(solution)/shard_map/all_to_all | solution.py:49
  205.6 2.2 fusion.20
  208.5 15.4 %all-to-all-done.3 = bf16[32,1,2,32,128]{4,3,2,1,0:T(8,128)(2,1)S(1)} async-done(((bf16[32,1,2,32,128]{4,3,2,1,0:T(8,128)(2,1)}), bf16[32,1,2,32,128]{4,3,2,1,0:T(8,128)(2,1)S(1)}, u32[]{:S(2)}, u32[]{:S(2)}) %all-to-all-start.3) | async-done | bytes 524320 | tf_op jit(solution)/shard_map/all_to_all | solution.py:49
  223.8 1.0 broadcast_in_dim.47
  224.8 4.9 %all-to-all-start.1 = ((bf16[32,1,2,32,128]{4,3,2,1,0:T(8,128)(2,1)}), bf16[32,1,2,32,128]{4,3,2,1,0:T(8,128)(2,1)}, u32[]{:S(2)}, u32[]{:S(2)}) async-start(bf16[32,1,2,32,128]{4,3,2,1,0:T(8,128)(2,1)} %broadcast_in_dim.47), calls=%async_computation.1 | async-start | bytes 1048576 | tf_op jit(solution)/shard_map/all_to_all | solution.py:49
  229.7 8.7 %fusion = bf16[1,128,64,128]{1,3,2,0:T(8,128)(2,1)S(1)} fusion(f32[1,128,64,128]{1,3,2,0:T(8,128)} %copy-done, f32[64,32,128]{2,1,0:T(8,128)} %fusion.20, f32[64,32,128]{2,1,0:T(8,128)S(1)} %bitcast.428), kind=kOutput, calls=%fused_computation.6 | convolution fusion | flops 404750336 | bytes 8388608 | tf_op jit(solution)/shard_map/rjpa,rjpb->rajb/dot_general | solution.py:73
  238.4 2.9 %copy.34 = bf16[1,128,8192]{2,1,0:T(8,128)(2,1)} copy(bf16[1,128,8192]{1,2,0:T(8,128)(2,1)S(1)} %bitcast.438) | data formatting | bytes 4194304
  241.3 4.6 %copy.25 = f32[128,8192]{0,1:T(8,128)} copy(bf16[128,8192]{1,0:T(8,128)(2,1)} %param.9) | data formatting | bytes 6291456 | tf_op jit(solution)/shard_map/reshape | solution.py:87
  246.7 0.6 gather_fusion.4
  247.8 1.2 bitcast_convert_fusion.1
  248.9 1.6 gather_fusion.2
  250.5 1.2 fusion.8
  251.8 2.6 fusion.11
  254.4 6.7 %fusion.60 = f32[64,128,128]{2,1,0:T(8,128)S(1)} fusion(f32[64,32,128]{2,1,0:T(8,128)S(1)} %fusion.11, f32[64,32,128]{2,1,0:T(8,128)S(1)} %bitcast.429), kind=kOutput, calls=%fused_computation.231 | convolution fusion | flops 402653184 | bytes 6291456 | tf_op jit(solution)/shard_map/rjpa,rjpb->rajb/dot_general | solution.py:73
  261.1 7.4 %fusion.1 = bf16[1,128,64,128]{1,3,2,0:T(8,128)(2,1)S(1)} fusion(f32[1,128,64,128]{1,3,2,0:T(8,128)S(1)} %bitcast.431, f32[64,128,128]{2,1,0:T(8,128)S(1)} %fusion.60, f32[64,32,128]{2,1,0:T(8,128)S(1)} %fusion.8, f32[64,32,128]{2,1,0:T(8,128)S(1)} %bitcast.430), kind=kOutput, calls=%fused_computation.8 | convolution fusion | flops 407896064 | bytes 12582912 | tf_op jit(solution)/shard_map/rjpa,rjpb->rajb/dot_general | solution.py:73
  268.5 2.9 %copy.33 = bf16[128,8192]{1,0:T(8,128)(2,1)} copy(bf16[128,8192]{0,1:T(8,128)(2,1)S(1)} %bitcast.437) | data formatting | bytes 4194304
  (102 shorter events, 39.5 us)
Async XLA Ops:
  10.0 2.7 copy-start.2
  66.2 7.9 %copy-start = (f32[1,128,64,128]{1,3,2,0:T(8,128)}, f32[1,128,64,128]{1,3,2,0:T(8,128)S(1)}, u32[]{:S(2)}) copy-start(f32[1,128,64,128]{1,3,2,0:T(8,128)S(1)} %fusion.3) | copy-start | bytes 12582916
  75.5 81.6 %copy-start.5 = (f32[1,2,32,128]{3,2,1,0:T(8,128)S(1)}, f32[1,2,32,128]{3,2,1,0:T(8,128)}, u32[]{:S(2)}) copy-start(f32[1,2,32,128]{3,2,1,0:T(8,128)} %param.15) | copy-start | bytes 98308
  75.5 81.6 %copy-start.6 = (f32[1,2,32,128]{3,2,1,0:T(8,128)S(1)}, f32[1,2,32,128]{3,2,1,0:T(8,128)}, u32[]{:S(2)}) copy-start(f32[1,2,32,128]{3,2,1,0:T(8,128)} %param.14) | copy-start | bytes 98308
  96.9 32.2 %all-to-all-start = ((bf16[32,1,2,32,128]{4,3,2,1,0:T(8,128)(2,1)}), bf16[32,1,2,32,128]{4,3,2,1,0:T(8,128)(2,1)S(1)}, u32[]{:S(2)}, u32[]{:S(2)}) async-start(bf16[32,1,2,32,128]{4,3,2,1,0:T(8,128)(2,1)} %constant_dynamic-update-slice_fusion), calls=%async_computation | async-start | bytes 1048576 | tf_op jit(solution)/shard_map/all_to_all | solution.py:24
  129.1 27.9 %all-to-all-start.2 = ((bf16[32,1,2,32,128]{4,3,2,1,0:T(8,128)(2,1)}), bf16[32,1,2,32,128]{4,3,2,1,0:T(8,128)(2,1)S(1)}, u32[]{:S(2)}, u32[]{:S(2)}) async-start(bf16[32,1,2,32,128]{4,3,2,1,0:T(8,128)(2,1)} %constant_dynamic-update-slice_fusion.32), calls=%async_computation.2 | async-start | bytes 1048576 | tf_op jit(solution)/shard_map/all_to_all | solution.py:24
  157.8 80.6 %copy-start.7 = (f32[1,2,32,128]{3,2,1,0:T(8,128)}, f32[1,2,32,128]{3,2,1,0:T(8,128)S(1)}, u32[]{:S(2)}) copy-start(f32[1,2,32,128]{3,2,1,0:T(8,128)S(1)} %get-tuple-element.34) | copy-start | bytes 98308
  157.8 80.6 %copy-start.8 = (f32[1,2,32,128]{3,2,1,0:T(8,128)}, f32[1,2,32,128]{3,2,1,0:T(8,128)S(1)}, u32[]{:S(2)}) copy-start(f32[1,2,32,128]{3,2,1,0:T(8,128)S(1)} %get-tuple-element.35) | copy-start | bytes 98308
  196.7 27.2 %all-to-all-start.3 = ((bf16[32,1,2,32,128]{4,3,2,1,0:T(8,128)(2,1)}), bf16[32,1,2,32,128]{4,3,2,1,0:T(8,128)(2,1)S(1)}, u32[]{:S(2)}, u32[]{:S(2)}) async-start(bf16[32,1,2,32,128]{4,3,2,1,0:T(8,128)(2,1)} %broadcast_in_dim.50), calls=%async_computation.3 | async-start | bytes 1048576 | tf_op jit(solution)/shard_map/all_to_all | solution.py:49
  223.8 1.0 copy-start.3
  224.8 23.0 %all-to-all-start.1 = ((bf16[32,1,2,32,128]{4,3,2,1,0:T(8,128)(2,1)}), bf16[32,1,2,32,128]{4,3,2,1,0:T(8,128)(2,1)}, u32[]{:S(2)}, u32[]{:S(2)}) async-start(bf16[32,1,2,32,128]{4,3,2,1,0:T(8,128)(2,1)} %broadcast_in_dim.47), calls=%async_computation.1 | async-start | bytes 1048576 | tf_op jit(solution)/shard_map/all_to_all | solution.py:49
  241.3 4.6 %copy-start.9 = (s32[1,64]{1,0:T(1,128)S(1)}, s32[1,64]{1,0:T(1,128)}, u32[]{:S(2)}) copy-start(s32[1,64]{1,0:T(1,128)} %param.13) | copy-start | bytes 772
  241.3 5.2 %copy-start.4 = (bf16[32,1,2,32,128]{4,3,2,1,0:T(8,128)(2,1)S(1)}, bf16[32,1,2,32,128]{4,3,2,1,0:T(8,128)(2,1)}, u32[]{:S(2)}) copy-start(bf16[32,1,2,32,128]{4,3,2,1,0:T(8,128)(2,1)} %copy-done.3) | copy-start | bytes 1572868
  251.7 9.3 %copy-start.1 = (f32[128,8192]{0,1:T(8,128)S(1)}, f32[128,8192]{0,1:T(8,128)}, u32[]{:S(2)}) copy-start(f32[128,8192]{0,1:T(8,128)} %copy.25) | copy-start | bytes 12582916
